TPU v7x, 32 devices: a whole 2x2x4 slice. The times are simulated.
32 devices in a mesh: dp: 4 (over z), expert: 2 (over x), shard: 4 (over y, core).
Axes of the slice: x: 2, y: 2, z: 4, core: 2. Of those that a mesh axis runs over, the one named last changes fastest.
Arguments:
- activations: bfloat16 [2, 2, 2048, 256], P(None, 'expert', ('dp', 'shard')), may hold values from -6 to 6
- out_grads: bfloat16 [2, 2, 2048, 14336], P(None, 'expert', ('dp', 'shard')), may hold values from -0.25 to 0.25
- weights: float32 [2, 2, 256, 14336], P(None, 'expert', ('dp', 'shard')), may hold values from -4 to 4
- shadow: float32 [2, 2, 256, 14336], P(None, 'expert', ('dp', 'shard')), may hold values from -4 to 4
- counts: int32 [2, 32, 2], P(None, ('dp', 'expert', 'shard')), may hold values from 1 to 1024, as said below
Outputs:
- new_weights: float32 [2, 2, 256, 14336], P(None, 'expert', ('dp', 'shard'))
- new_shadow: float32 [2, 2, 256, 14336], P(None, 'expert', ('dp', 'shard'))
Inputs may be any that keep to these rules, and one draw needn't show every extreme that they name: `counts`: loads differ between the experts of a layer.
All inputs are finite; a program needn't handle non-finite values.
Results may differ from a plain program's by a relative error of at most 0.0003.
Values sent between devices are 32-bit elements; how exact they have to be, the bound alone decides.
A program may use at most 128 MiB of HBM per device.

v0:
```python
from functools import partial

import jax
import jax.numpy as jnp
from jax import lax
from jax.sharding import PartitionSpec as P

LAYERS = 2


step_size = 0.5
clip_level = 1.0


def partial_rows(inputs, cotangent, start, count):
    return lax.dot_general(
        inputs, cotangent, (((0,), (0,)), ((), ())), preferred_element_type=jnp.float32
    )


def on_device(activations, out_grads, weights, shadow, counts):
    experts = counts.shape[-1]
    own_slot = (jnp.arange(experts) == lax.axis_index("expert")).astype(jnp.float32)
    own_rows = weights.shape[2]
    load_totals = lax.psum(counts[:, 0, :], ("dp", "expert", "shard"))
    all_weights = []
    all_shadow = []
    for layer_index in range(LAYERS):
        inputs = activations[layer_index, 0]
        cotangent = out_grads[layer_index, 0]
        term = partial(partial_rows, inputs, cotangent)
        summed = lax.psum_scatter(
            term(jnp.int32(0), lax.axis_size(("dp", "shard")) * own_rows),
            ("dp", "shard"),
            scatter_dimension=0,
            tiled=True,
        )
        squares = jnp.sum(summed * summed)
        loads = load_totals[layer_index].astype(jnp.float32)
        total_squares = lax.psum(squares, ("dp", "shard"))
        own_load = jnp.sum(loads * own_slot)
        mean_load = jnp.mean(loads)
        numel = inputs.shape[1] * cotangent.shape[1]
        root_mean = jnp.sqrt(total_squares / numel)
        factor = (
            step_size * (own_load / mean_load) * clip_level / jnp.maximum(root_mean, clip_level)
        )
        updated = weights[layer_index, 0] - factor * summed
        beta = own_load / (own_load + mean_load)
        previous = shadow[layer_index, 0]
        all_weights.append(updated)
        all_shadow.append(previous + beta * (updated - previous))
    return (jnp.stack(all_weights)[:, None], jnp.stack(all_shadow)[:, None])


def solution(mesh):
    in_specs = (
        P(None, "expert", ("dp", "shard"), None),
        P(None, "expert", ("dp", "shard"), None),
        P(None, "expert", ("dp", "shard"), None),
        P(None, "expert", ("dp", "shard"), None),
        P(None, ("dp", "expert", "shard"), None),
    )
    out_specs = (P(None, "expert", ("dp", "shard"), None), P(None, "expert", ("dp", "shard"), None))
    return jax.shard_map(
        on_device, mesh=mesh, in_specs=in_specs, out_specs=out_specs, check_vma=False
    )
```

profile of v0, /device:TPU:0, one launch (start us, length us, event | category | flops | bytes accessed | tf_op | source)
XLA Modules:
  0.0 370.9 jit_solution(8719449823756068406)
XLA Ops:
  7.2 0.0 reduce-scatter.5.cloned.1.call-start
  7.2 9.4 %fusion = f32[256,14336]{1,0:T(8,128)} fusion(bf16[2,1,128,14336]{3,2,1,0:T(8,128)(2,1)} %param.6, bf16[2,1,128,256]{3,2,1,0:T(8,128)(2,1)} %param.5), kind=kOutput, calls=%fused_computation | convolution fusion | flops 939524096 | bytes 18415616 | tf_op jit(solution)/shard_map/dot_general | solution.py:16
  16.6 0.0 copy-start.1
  16.6 0.0 reduce-scatter.5.cloned.1.call-update
  16.6 0.0 reduce-scatter.3.cloned.1.call-start
  16.7 0.8 copy-done.1
  17.5 10.1 %fusion.2 = f32[256,14336]{1,0:T(8,128)} fusion(bf16[2,1,128,14336]{3,2,1,0:T(8,128)(2,1)} %param.6, bf16[2,1,128,256]{3,2,1,0:T(8,128)(2,1)S(1)} %copy-done.1), kind=kOutput, calls=%fused_computation.2 | convolution fusion | flops 939524096 | bytes 18415616 | tf_op jit(solution)/shard_map/dot_general | solution.py:16
  27.6 0.0 copy-start.2
  27.6 0.0 copy-start
  27.6 0.0 reduce-scatter.3.cloned.1.call-update
  27.7 0.7 copy-done.2
  28.3 46.0 %psum.21 = s32[2,2]{1,0:T(2,128)S(1)} all-reduce(s32[2,2]{1,0:T(2,128)S(1)} %bitcast.63), channel_id=1, replica_groups=mesh['dp'=4,'expert'=2,'shard'=4] {'dp','expert','shard'}, use_global_device_ids=true, to_apply=%region_0.0 | all-reduce | flops 4 | bytes 32 | tf_op jit(solution)/shard_map/psum | solution.py:25
  74.3 0.7 convert_reduce_fusion.1
  75.7 0.6 fusion.16
  80.2 89.7 %reduce-scatter.5.cloned.1.call-done = f32[16,14336]{1,0:T(8,128)} async-done(((f32[256,14336]{1,0:T(8,128)}), f32[16,14336]{1,0:T(8,128)}) %reduce-scatter.5.cloned.1.call-update) | async-done | bytes 917520 | tf_op jit(solution)/shard_map/reduce_scatter | solution.py:32
  169.9 2.0 multiply_reduce_fusion
  171.9 151.3 %reduce-scatter.3.cloned.1.call-done = f32[16,14336]{1,0:T(8,128)} async-done(((f32[256,14336]{1,0:T(8,128)}), f32[16,14336]{1,0:T(8,128)}) %reduce-scatter.3.cloned.1.call-update) | async-done | bytes 917520 | tf_op jit(solution)/shard_map/reduce_scatter | solution.py:32
  323.2 2.1 multiply_reduce_fusion.1
  325.9 32.2 %all-reduce = (f32[]{:T(128)}, f32[]{:T(128)}) all-reduce(f32[]{:T(128)} %multiply_reduce_fusion, f32[]{:T(128)} %multiply_reduce_fusion.1), channel_id=1, replica_groups=mesh['dp'=4,'expert'=2,'shard'=4] {'dp','shard'}, use_global_device_ids=true, to_apply=%region_10.0 | all-reduce | flops 2 | bytes 16 | tf_op jit(solution)/shard_map/psum | solution.py:40
  359.6 0.0 copy-done
  359.6 2.4 fusion.9
  362.0 2.1 maximum_bitcast_fusion
Async XLA Ops:
  7.2 162.7 %reduce-scatter.5.cloned.1.call-start = ((), (), s32[]{:S(2)}) async-start(), calls=%async_computation.3 | async-start | bytes 15597568 | tf_op jit(solution)/shard_map/reduce_scatter | solution.py:32
  16.6 0.9 copy-start.1
  16.6 306.6 %reduce-scatter.3.cloned.1.call-start = ((), (), s32[]{:S(2)}) async-start(), calls=%async_computation.2 | async-start | bytes 15597568 | tf_op jit(solution)/shard_map/reduce_scatter | solution.py:32
  27.6 0.7 copy-start.2
  27.6 332.0 %copy-start = (f32[2,1,16,14336]{3,2,1,0:T(8,128)S(1)}, f32[2,1,16,14336]{3,2,1,0:T(8,128)}, u32[]{:S(2)}) copy-start(f32[2,1,16,14336]{3,2,1,0:T(8,128)} %param.8) | copy-start | bytes 5505028
Sparse Core Ops, SparseCore 0:
  16.8 153.1 reduce-scatter.4
  174.0 149.1 reduce-scatter.2
where the time goes:
time: 371 us
  waiting for transfers between devices  241 us (65%)
  blocking collectives  78.2 us (21%)
  between operations  20.8 us (6%)
  matrix products  19.5 us (5%)
  other arithmetic  9.86 us (3%)
    reduce_scatter x2, waiting for transfers between devices, on_device(): lax.psum_scatter(term(jnp.int32(0), lax.axis_size(('dp', 'shard')) * own_...  241 us
    psum x1, blocking collectives, on_device(): load_totals = lax.psum(counts[:, 0, :], ('dp', 'expert', 'shard'))  46 us
    psum x1, blocking collectives, on_device(): total_squares = lax.psum(squares, ('dp', 'shard'))  32.2 us
    dot_general x2, matrix products, partial_rows(): lax.dot_general(inputs, cotangent, (((0,), (0,)), ((), ())), preferred_el...  19.5 us
  transfers between devices with their start and end apart: 2, of which 2 were waited for; matrix products, arithmetic and copies ran while one was open for 4% of the time, Pallas kernels for 0%

commit v1 on v0

v1 whole, which is shorter than its diff:
```python
import functools

import jax
import jax.numpy as jnp
from jax import lax
from jax.experimental import pallas as pl
from jax.experimental.pallas import tpu as pltpu
from jax.sharding import PartitionSpec as P

step_size = 0.5
clip_level = 1.0
CORES = 2
SLOTS = 4
LAG = 3
COLS = 256
MESH = pl.DeviceIdType.MESH


def kernel(
    dims, rows_ref, cot_ref, cnt_ref, out_ref, stat_ref,
    merged, from_y, from_z, from_zx, late_y, staged, squares, seen, message, gathered,
    core_send, core_recv, y_send, y_recv, z_send, z_recv, zx_send, zx_recv,
    late_send, late_recv, cnt_send, cnt_recv, all_send, all_recv,
):
    line, experts, shards, layers, per_layer, width, rows, numel = dims
    group = line * shards
    half = line * rows
    chunks = layers * per_layer
    z, e, s = lax.axis_index("dp"), lax.axis_index("expert"), lax.axis_index("shard")
    y, c = s // CORES, s % CORES
    me = z * shards + s
    core_peer = {"shard": y * CORES + (1 - c)}
    y_peer = {"shard": (1 - y) * CORES + c}
    own, other = y * half, (1 - y) * half

    def group_peer(d):
        p = lax.rem(me + d, group)
        return p, {"dp": p // shards, "shard": p % shards}

    def remote(src, dst, send, recv, device):
        return pltpu.make_async_remote_copy(
            src_ref=src, dst_ref=dst, send_sem=send, recv_sem=recv,
            device_id=device, device_id_type=MESH,
        )

    barrier = pltpu.get_barrier_semaphore()
    for d in range(1, group):
        pl.semaphore_signal(barrier, inc=1, device_id=group_peer(d)[1], device_id_type=MESH)
    for d in range(1, experts):
        pl.semaphore_signal(
            barrier, inc=1, device_id={"expert": lax.rem(e + d, experts)}, device_id_type=MESH
        )
    pl.semaphore_wait(barrier, group + experts - 2)

    def count_copy(d, sender):
        return remote(
            cnt_ref, seen.at[sender], cnt_send.at[d], cnt_recv.at[sender],
            {"expert": lax.rem(e + d, experts)},
        )

    for d in range(1, experts):
        count_copy(d, e).start()
    squares[...] = jnp.zeros_like(squares)

    def place(k):
        return k // per_layer, k % per_layer

    def when_chunk(k, body):
        pl.when((k >= 0) & (k < chunks))(lambda: body(k))

    def core_copy(k):
        return remote(
            staged.at[k % SLOTS], merged.at[k], core_send.at[k % SLOTS], core_recv.at[k], core_peer
        )

    def y_copy(k):
        return remote(
            merged.at[k, pl.ds(pl.multiple_of(other, 8), half)], from_y.at[k],
            y_send.at[k], y_recv.at[k], y_peer,
        )

    def late_copy(layer):
        k = layer * per_layer
        return remote(
            merged.at[k, pl.ds(pl.multiple_of(other + z * rows, 8), rows)], late_y.at[layer],
            late_send.at[layer], late_recv.at[layer], y_peer,
        )

    def product(layer, q, core, i):
        at = pl.ds(pl.multiple_of(q * width + i * COLS, 128), COLS)
        return jnp.dot(
            rows_ref[layer, core], cot_ref[layer, :, at], preferred_element_type=jnp.float32
        )

    def stage_partner(k):
        layer, q = place(k)
        pl.when(k >= SLOTS)(lambda: core_copy(k - SLOTS).wait_send())

        def tile(i, _):
            at = pl.ds(pl.multiple_of(i * COLS, 128), COLS)
            staged[k % SLOTS, :, at] = product(layer, q, 1 - c, i)
            return 0

        lax.fori_loop(0, width // COLS, tile, 0)
        core_copy(k).start()

    def merge_core(k):
        layer, q = place(k)
        core_copy(k).wait_recv()

        def tile(i, _):
            at = pl.ds(pl.multiple_of(i * COLS, 128), COLS)
            merged[k, :, at] = merged[k, :, at] + product(layer, q, c, i)
            return 0

        lax.fori_loop(0, width // COLS, tile, 0)
        pl.when(q > 0)(lambda: y_copy(k).start())

    def merge_y(k):
        @pl.when(k % per_layer > 0)
        def _():
            y_copy(k).wait_recv()
            at = pl.ds(pl.multiple_of(own, 8), half)
            merged[k, at, :] = merged[k, at, :] + from_y[k]

    def block(k, base, b):
        return merged.at[k, pl.ds(pl.multiple_of(base + b * rows, 8), rows)]

    def z_copy(k, base, b, slot, device, extra):
        layer = k // per_layer
        if extra:
            return remote(
                block(k, base, b), from_zx.at[layer, slot], zx_send.at[layer, b],
                zx_recv.at[layer, slot], device,
            )
        return remote(
            block(k, base, b), from_z.at[k, slot], z_send.at[k, b], z_recv.at[k, slot], device
        )

    def arrived(k, slot, extra):
        return from_zx[k // per_layer, slot] if extra else from_z[k, slot]

    def add_arrived(k, base, b, slot, extra):
        z_copy(k, base, b, slot, {"dp": z}, extra).wait_recv()
        ref = block(k, base, b)
        ref[...] = ref[...] + arrived(k, slot, extra)

    def to_right(k, base, extra):
        for b in reversed(range(1, line)):
            @pl.when(z < b)
            def _():
                pl.when(z > 0)(lambda: add_arrived(k, base, b, b + 1, extra))
                z_copy(k, base, b, b + 1, {"dp": z + 1}, extra).start()

    def to_left(k, base, extra):
        for b in range(line - 1):
            @pl.when(z > b)
            def _():
                pl.when(z < line - 1)(lambda: add_arrived(k, base, b, b, extra))
                z_copy(k, base, b, b, {"dp": z - 1}, extra).start()

    def both_halves(pass_one):
        def body(k):
            pl.when(k % per_layer == 0)(lambda: pass_one(k, other, True))
            pass_one(k, own, False)
        return body

    def put(k, values):
        layer, q = place(k)
        out_ref[layer, :, pl.ds(pl.multiple_of(q * width, 128), width)] = values
        squares[layer] = squares[layer] + values * values

    def finish_one(k, base, extra):
        pl.when(z > 0)(lambda: add_arrived(k, base, z, z + 1, extra))
        pl.when(z < line - 1)(lambda: add_arrived(k, base, z, z, extra))
        if extra:
            late_copy(k // per_layer).start()
        else:
            pl.when(k % per_layer > 0)(lambda: put(k, block(k, base, z)[...]))

    def step(t, _):
        when_chunk(t, stage_partner)
        when_chunk(t - 1, merge_core)
        when_chunk(t - LAG, merge_y)
        back = line - 1 - z
        when_chunk(t - LAG - z, both_halves(to_right))
        when_chunk(t - LAG - back, both_halves(to_left))
        when_chunk(t - LAG - jnp.maximum(z, back), both_halves(finish_one))
        return 0

    lax.fori_loop(0, chunks + LAG + line - 1, step, 0)

    for layer in range(layers):
        late_copy(layer).wait_recv()
        put(layer * per_layer, block(layer * per_layer, own, z)[...] + late_y[layer])

    totals = cnt_ref[...]
    for d in range(1, experts):
        sender = lax.rem(e + d, experts)
        count_copy(d, sender).wait_recv()
        totals = totals + seen[sender]
    row = lax.broadcasted_iota(jnp.int32, totals.shape, 0)
    lane = lax.broadcasted_iota(jnp.int32, totals.shape, 1)
    for layer in range(layers):
        share = jnp.sum(jnp.sum(squares[layer], axis=0, keepdims=True), axis=1, keepdims=True)
        totals = jnp.where(row == layer, share, totals)
    message[...] = totals
    gathered[me] = totals

    def all_copy(d, sender):
        return remote(
            message, gathered.at[sender], all_send.at[d], all_recv.at[sender], group_peer(d)[1]
        )

    for d in range(1, group):
        all_copy(d, me).start()
    for d in range(1, group):
        all_copy(d, group_peer(d)[0]).wait_recv()
    total = gathered[0]
    for p in range(1, group):
        total = total + gathered[p]
    stats = jnp.zeros_like(total)
    for layer in range(layers):
        loads = total[layers + layer:layers + layer + 1, :]
        spot = lane[:1]
        own_load = jnp.sum(jnp.where(spot == e, loads, 0.0), axis=1, keepdims=True)
        mean_load = jnp.sum(jnp.where(spot < experts, loads, 0.0), axis=1, keepdims=True) / experts
        root_mean = jnp.sqrt(total[layer:layer + 1, :1] / numel)
        factor = (
            step_size * (own_load / mean_load) * clip_level / jnp.maximum(root_mean, clip_level)
        )
        beta = own_load / (own_load + mean_load)
        stats = jnp.where(row == layer, factor, stats)
        stats = jnp.where(row == layers + layer, beta, stats)
    stat_ref[...] = stats

    for d in range(1, group):
        all_copy(d, me).wait_send()
    for d in range(1, experts):
        count_copy(d, e).wait_send()
    for k in range(chunks - min(SLOTS, chunks), chunks):
        core_copy(k).wait_send()

    def drain(k, _):
        pl.when(k % per_layer > 0)(lambda: y_copy(k).wait_send())
        for b in range(line):
            pl.when(z != b)(lambda: z_copy(k, own, b, b, {"dp": z}, False).wait_send())
        return 0

    lax.fori_loop(0, chunks, drain, 0)
    for layer in range(layers):
        late_copy(layer).wait_send()
        for b in range(line):
            pl.when(z != b)(
                lambda: z_copy(layer * per_layer, other, b, b, {"dp": z}, True).wait_send()
            )


def on_device(sizes, activations, out_grads, weights, shadow, counts):
    line, experts, shards = sizes
    layers, _, tokens, all_rows = activations.shape
    ff, rows = out_grads.shape[3], weights.shape[2]
    assert shards == 2 * CORES and 2 * layers <= 8
    units = ff // 128
    per_layer = next(p for p in range(6, units + 1) if units % p == 0 and units // p % 2 == 0)
    width = ff // per_layer
    chunks = layers * per_layer
    half = line * rows
    group = line * shards
    acts = activations[:, 0].reshape(layers, tokens, line, shards // CORES, CORES, rows)
    acts = acts.transpose(0, 4, 3, 2, 5, 1).reshape(layers, CORES, all_rows // CORES, tokens)
    tile = jnp.pad(
        counts[:, 0, :].astype(jnp.float32), ((layers, 8 - 2 * layers), (0, 128 - experts))
    )
    f32 = jnp.float32
    dma = pltpu.SemaphoreType.DMA
    vmem = pl.BlockSpec(memory_space=pltpu.VMEM)
    dims = (line, experts, shards, layers, per_layer, width, rows, all_rows * ff)
    summed, stats = pl.pallas_call(
        functools.partial(kernel, dims),
        out_shape=(
            jax.ShapeDtypeStruct((layers, rows, ff), f32), jax.ShapeDtypeStruct((8, 128), f32)
        ),
        in_specs=[vmem] * 3,
        out_specs=(vmem, vmem),
        scratch_shapes=[
            pltpu.VMEM((chunks, 2 * half, width), f32),
            pltpu.VMEM((chunks, half, width), f32),
            pltpu.VMEM((chunks, line + 1, rows, width), f32),
            pltpu.VMEM((layers, line + 1, rows, width), f32),
            pltpu.VMEM((layers, rows, width), f32),
            pltpu.VMEM((SLOTS, 2 * half, width), f32),
            pltpu.VMEM((layers, rows, width), f32),
            pltpu.VMEM((experts, 8, 128), f32),
            pltpu.VMEM((8, 128), f32),
            pltpu.VMEM((group, 8, 128), f32),
            dma((SLOTS,)), dma((chunks,)), dma((chunks,)), dma((chunks,)),
            dma((chunks, line)), dma((chunks, line + 1)),
            dma((layers, line)), dma((layers, line + 1)),
            dma((layers,)), dma((layers,)), dma((experts,)), dma((experts,)),
            dma((group,)), dma((group,)),
        ],
        compiler_params=pltpu.CompilerParams(
            collective_id=0, has_side_effects=True, vmem_limit_bytes=62 * 1024 * 1024
        ),
        name="reduce_gradient",
    )(acts, out_grads[:, 0], tile)
    factor = stats[:layers, 0][:, None, None]
    beta = stats[layers:2 * layers, 0][:, None, None]
    updated = weights[:, 0] - factor * summed
    previous = shadow[:, 0]
    return updated[:, None], (previous + beta * (updated - previous))[:, None]


def solution(mesh):
    rows = P(None, "expert", ("dp", "shard"), None)
    in_specs = (rows, rows, rows, rows, P(None, ("dp", "expert", "shard"), None))
    sizes = tuple(mesh.shape[a] for a in ("dp", "expert", "shard"))
    return jax.shard_map(
        functools.partial(on_device, sizes), mesh=mesh, in_specs=in_specs,
        out_specs=(rows, rows), check_vma=False,
    )
```

time: 371 us -> 191 us (0.51)
  waiting for transfers between devices: 241 us -> 0 us
  Pallas kernels: 0 us -> 182 us
  blocking collectives: 78.2 us -> 0 us
  between operations: 20.8 us -> 0.65 us
  matrix products: 19.5 us -> 0 us
  other arithmetic: 9.86 us -> 4.98 us
    reduce_scatter x2 -> x0, waiting for transfers between devices: 241 us -> none  [on_device(): lax.psum_scatter(term(jnp.int32(0), lax.axis_size(('dp', 'shard')) * own_...]
    pallas_call x0 -> x1, Pallas kernels: none -> 182 us  [on_device(): pl.pallas_call(functools.partial(kernel, dims), out_shape=(jax.ShapeDtype...]
    psum x2 -> x0, blocking collectives: 78.2 us -> none  [the longest x1 46 us: on_device(): load_totals = lax.psum(counts[:, 0, :], ('dp', 'expert', 'shard'))]
    dot_general x2 -> x0, matrix products: 19.5 us -> none  [partial_rows(): lax.dot_general(inputs, cotangent, (((0,), (0,)), ((), ())), preferred_el...]
    reduce_sum x4 -> x0, other arithmetic: 5.41 us -> none  [the longest x2 4.12 us: on_device(): squares = jnp.sum(summed * summed)]
  transfers between devices with their start and end apart: 2 -> 0, of which waited for: 2 -> 0; matrix products, arithmetic and copies ran while one was open for 4% -> 0% of each run, Pallas kernels for 0% -> 0%
where the time goes in v1:
time: 191 us
  Pallas kernels  182 us (95%)
  other arithmetic  4.98 us (3%)
  local copies, waits for them, and re-layouts  3.2 us (2%)
    pallas_call x1, Pallas kernels, on_device(): pl.pallas_call(functools.partial(kernel, dims), out_shape=(jax.ShapeDtype...  182 us
    unnamed x1, other arithmetic  4.29 us

profile of v1, /device:TPU:0, one launch (start us, length us, event | category | flops | bytes accessed | tf_op | source)
XLA Modules:
  0.0 191.1 jit_solution(6211625333718271075)
XLA Ops:
  0.6 0.7 convert_element_type.8
  1.3 0.6 pad.4.cnt_ref
  1.9 1.0 copy.10
  2.9 0.7 copy.11
  3.6 0.0 copy-start
  3.6 182.3 %reduce_gradient.1 = (f32[2,16,14336]{2,1,0:T(8,128)}, f32[8,128]{1,0:T(8,128)}) custom-call(bf16[2,2,128,128]{3,2,1,0:T(8,128)(2,1)} %bitcast.30, bf16[2,128,14336]{2,1,0:T(8,128)(2,1)} %bitcast.29, f32[8,128]{1,0:T(8,128)} %pad.4.cnt_ref), custom_call_target="tpu_custom_call" | custom-call | tf_op jit(solution)/shard_map/reduce_gradient/pallas_call | solution.py:279
  185.9 0.9 slice_reduce_fusion
  186.8 0.0 copy-done
  186.8 4.3 %fusion.1 = (f32[2,1,16,14336]{3,2,1,0:T(8,128)}, f32[2,1,16,14336]{3,2,1,0:T(8,128)}) fusion(f32[2,1,16,14336]{3,2,1,0:T(8,128)S(1)} %copy-done, f32[2]{0:T(128)S(1)} %get-tuple-element.10, f32[2,16,14336]{2,1,0:T(8,128)} %get-tuple-element.5, f32[2]{0:T(128)S(1)} %get-tuple-element.11, f32[2,1,16,14336]{3,2,1,0:T(8,128)} %param.7), kind=kLoop, calls=%fused_computation.3 | loop fusion | flops 2293760 | bytes 9175056
Async XLA Ops:
  3.6 183.2 %copy-start = (f32[2,1,16,14336]{3,2,1,0:T(8,128)S(1)}, f32[2,1,16,14336]{3,2,1,0:T(8,128)}, u32[]{:S(2)}) copy-start(f32[2,1,16,14336]{3,2,1,0:T(8,128)} %param.8) | copy-start | bytes 5505028
